TPU v7x, 512 devices: a 4x2x32 block of a 4x8x32 slice. The times are simulated.
512 devices in a mesh: member: 2 (over y), tile: 32 (over z), row: 4 (over x), lev: 2 (over core).
Axes of the slice: x: 4, y: 2, z: 32, core: 2. Of those that a mesh axis runs over, the one named last changes fastest.
The devices are a block of a 4x8x32 slice.
Arguments:
- thickness: float32 [128, 512, 512], P(('member', 'lev'), 'tile', 'row'), parts along dimension 0, may hold values from 0.24 to 14.91
- zonal_wind: float32 [128, 512, 512], P(('member', 'lev'), 'tile', 'row'), parts along dimension 0, may hold values from -1.8 to 1.8
- merid_wind: float32 [128, 512, 512], P(('member', 'lev'), 'tile', 'row'), parts along dimension 0, may hold values from -1.8 to 1.8
- pert_codes: int32 [1024, 512], P(('member', 'tile'), 'row'), parts along dimension 0, may hold values from 0 to 1073741823
Outputs:
- thick_out: float32 [128, 512, 512], P(('member', 'lev'), 'tile', 'row'), parts along dimension 0
- zonal_out: float32 [128, 512, 512], P(('member', 'lev'), 'tile', 'row'), parts along dimension 0
- merid_out: float32 [128, 512, 512], P(('member', 'lev'), 'tile', 'row'), parts along dimension 0
There are 2 independent parts, one for each index of `member`. A program takes and returns all parts, laid end to end along the dimension named above; each array names one. Nothing has to cross between parts.
All inputs are finite; a program needn't handle non-finite values.
Results may differ from a plain program's by a relative error of at most 0.0003.
Values sent between devices are 32-bit elements; how exact they have to be, the bound alone decides.
A program may use at most 64 MiB of HBM per device.

v0:
```python
import jax
import jax.numpy as jnp
from jax import lax
from jax.sharding import PartitionSpec as P

NSUB = 4


CFL_NUMBER = 0.8


def one_axis_at_a_time(shard, axes):
    for axis in axes:
        shard = lax.pmax(shard, axis)
    return shard


def over_axes(shard, axes):
    for axis in axes:
        shard = lax.psum(shard, axis)
    return shard


def padded(block, sides, width):
    for axis, dim in sides:
        count = lax.axis_size(axis)
        forward = [(i, i + 1) for i in range(count - 1)]
        forward.append((count - 1, 0))
        backward = [(target, source) for source, target in forward]
        low = lax.ppermute(
            lax.slice_in_dim(block, block.shape[dim] - width, None, axis=dim), axis, forward
        )
        high = lax.ppermute(lax.slice_in_dim(block, 0, width, axis=dim), axis, backward)
        block = jnp.concatenate([low, block, high], axis=dim)
    return block


def joined_along(pieces, dim):
    pieces = jnp.moveaxis(pieces, 0, dim)
    dims = pieces.shape
    return pieces.reshape(*dims[:dim], dims[dim] * dims[dim + 1], *dims[dim + 2 :])


def sent_to_all(shard, axis):
    length = lax.axis_size(axis)
    return lax.all_to_all(
        jnp.broadcast_to(shard[None], (length, *shard.shape)), axis, 0, 0, tiled=True
    )


def gathered_copies(shard, axis, dim):
    return joined_along(sent_to_all(shard, axis), dim)


def advance(stacked, half_step):
    height = stacked[0]
    zonal = stacked[1]
    merid = stacked[2]
    zonal_new = zonal[:, 1:-1, 1:-1] - half_step * (height[:, 2:, 1:-1] - height[:, :-2, 1:-1])
    merid_new = merid[:, 1:-1, 1:-1] - half_step * (height[:, 1:-1, 2:] - height[:, 1:-1, :-2])
    centre = height[:, 1:-1, 1:-1]
    flux_east = centre * zonal_new
    flux_north = centre * merid_new
    height_new = centre[:, 1:-1, 1:-1] - half_step * (
        flux_east[:, 2:, 1:-1]
        - flux_east[:, :-2, 1:-1]
        + (flux_north[:, 1:-1, 2:] - flux_north[:, 1:-1, :-2])
    )
    return jnp.stack([height_new, zonal_new[:, 1:-1, 1:-1], merid_new[:, 1:-1, 1:-1]])


def remap_columns(columns, first, count):
    height = columns[0]
    zonal = columns[1]
    merid = columns[2]
    levels = height.shape[0]
    total = jnp.sum(height, 0)
    tops = jnp.cumsum(height, 0) - height
    marks = (first + jnp.arange(count + 1)).astype(jnp.float32)
    targets = total[None] * (marks / levels)[:, None, None]
    zonal_sum = jnp.zeros(targets.shape, jnp.float32)
    merid_sum = jnp.zeros(targets.shape, jnp.float32)
    for block in range(levels // 8):
        lower = block * 8
        upper = lower + 8
        over = jnp.clip(targets[None] - tops[lower:upper, None], 0.0, height[lower:upper, None])
        zonal_sum = zonal_sum + jnp.sum(zonal[lower:upper, None] * over, 0)
        merid_sum = merid_sum + jnp.sum(merid[lower:upper, None] * over, 0)
    layer = total / levels
    thick_new = jnp.broadcast_to(layer, (count,) + layer.shape)
    zonal_new = (zonal_sum[1:] - zonal_sum[:-1]) / layer
    merid_new = (merid_sum[1:] - merid_sum[:-1]) / layer
    return jnp.stack([thick_new, zonal_new, merid_new])


def local(thickness, zonal_wind, merid_wind, pert_codes):
    bump = 2.0 * (pert_codes % 4096).astype(jnp.float32) / 4095.0
    raised = thickness + bump[None]
    local_peak = jnp.max(raised)
    base_mass = jnp.sum(thickness)
    raised_mass = jnp.sum(raised)
    peak = one_axis_at_a_time(local_peak, ("tile", "row", "lev"))
    base_total, raised_total = (
        over_axes(base_mass, ("tile", "row", "lev")),
        over_axes(raised_mass, ("tile", "row", "lev")),
    )
    height = raised * (base_total / raised_total)
    half_step = 0.5 * CFL_NUMBER / jnp.sqrt(peak)
    state = jnp.stack([height, zonal_wind, merid_wind])
    state = padded(state, (("tile", 2), ("row", 3)), 2 * NSUB)
    for substep in range(NSUB):
        state = advance(state, half_step)
    levels_here = state.shape[1]
    columns = gathered_copies(state, "lev", 1)
    result = remap_columns(columns, lax.axis_index("lev") * levels_here, levels_here)
    return (result[0], result[1], result[2])


def solution(mesh):
    in_specs = (
        P(("member", "lev"), "tile", "row"),
        P(("member", "lev"), "tile", "row"),
        P(("member", "lev"), "tile", "row"),
        P(("member", "tile"), "row"),
    )
    out_specs = (
        P(("member", "lev"), "tile", "row"),
        P(("member", "lev"), "tile", "row"),
        P(("member", "lev"), "tile", "row"),
    )
    return jax.shard_map(local, mesh=mesh, in_specs=in_specs, out_specs=out_specs, check_vma=False)
```

profile of v0, /device:TPU:33, one launch (start us, length us, event | category | flops | bytes accessed | tf_op | source)
XLA Modules:
  0.0 252.3 jit_solution(18031665177296941275)
XLA Ops:
  1.4 1.6 add_reduce_fusion
  3.0 83.6 %all-reduce = (f32[]{:T(128)}, f32[]{:T(128)}) all-reduce(f32[]{:T(128)} %get-tuple-element.33, f32[]{:T(128)} %get-tuple-element.32), channel_id=1, replica_groups=mesh['member'=2,'tile'=32,'row'=4,'lev'=2] {'tile'}, use_global_device_ids=true, to_apply=%region_1.2 | all-reduce | flops 2 | bytes 16 | tf_op jit(solution)/shard_map/psum | solution.py:20
  86.7 9.5 %all-reduce.1 = (f32[]{:T(128)}, f32[]{:T(128)}) all-reduce(f32[]{:T(128)} %get-tuple-element.34, f32[]{:T(128)} %get-tuple-element.35), channel_id=1, replica_groups=mesh['member'=2,'tile'=32,'row'=4,'lev'=2] {'row'}, use_global_device_ids=true, to_apply=%region_2.3 | all-reduce | flops 2 | bytes 16 | tf_op jit(solution)/shard_map/psum | solution.py:20
  96.2 19.4 %all-reduce.2 = (f32[]{:T(128)}, f32[]{:T(128)}) all-reduce(f32[]{:T(128)} %get-tuple-element.36, f32[]{:T(128)} %get-tuple-element.37), channel_id=1, replica_groups=mesh['member'=2,'tile'=32,'row'=4,'lev'=2] {'lev'}, use_global_device_ids=true, to_apply=%region_3.4 | all-reduce | flops 2 | bytes 16 | tf_op jit(solution)/shard_map/psum | solution.py:20
  119.0 2.0 collective-permute-start
  121.0 4.6 %collective-permute-start.1 = (f32[3,32,8,128]{3,2,1,0:T(8,128)S(1)}, f32[3,32,8,128]{3,2,1,0:T(8,128)}, u32[]{:S(2)}, u32[]{:S(2)}) collective-permute-start(f32[3,32,8,128]{3,2,1,0:T(8,128)S(1)} %get-tuple-element.74), channel_id=1, source_target_pairs={{8,0},{16,8},{24,16},{32,24},{40,32},{48,40},{56,48},{64,56},{72,6... | collective-permute-start | bytes 1179656 | tf_op jit(solution)/shard_map/ppermute | solution.py:33
  125.6 46.2 %pmax.21 = f32[]{:T(128)} all-reduce(f32[]{:T(128)} %get-tuple-element.31), channel_id=1, replica_groups=mesh['member'=2,'tile'=32,'row'=4,'lev'=2] {'tile'}, use_global_device_ids=true, to_apply=%region_9.10 | all-reduce | flops 1 | bytes 8 | tf_op jit(solution)/shard_map/pmax | solution.py:14
  171.8 6.7 %pmax.22 = f32[]{:T(128)} all-reduce(f32[]{:T(128)} %pmax.21), channel_id=1, replica_groups=mesh['member'=2,'tile'=32,'row'=4,'lev'=2] {'row'}, use_global_device_ids=true, to_apply=%region_10.11 | all-reduce | flops 1 | bytes 8 | tf_op jit(solution)/shard_map/pmax | solution.py:14
  178.5 18.6 %pmax.23 = f32[]{:T(128)} all-reduce(f32[]{:T(128)} %pmax.22), channel_id=1, replica_groups=mesh['member'=2,'tile'=32,'row'=4,'lev'=2] {'lev'}, use_global_device_ids=true, to_apply=%region_11.12 | all-reduce | flops 1 | bytes 8 | tf_op jit(solution)/shard_map/pmax | solution.py:14
  197.8 1.3 pad_maximum_fusion.1
  200.9 3.6 %collective-permute-start.2 = (f32[3,32,32,8]{2,3,1,0:T(8,128)}, f32[3,32,32,8]{2,3,1,0:T(8,128)S(1)}, u32[]{:S(2)}, u32[]{:S(2)}) collective-permute-start(f32[3,32,32,8]{2,3,1,0:T(8,128)} %copy.20), channel_id=1, source_target_pairs={{0,2},{2,4},{4,6},{6,0},{1,3},{3,5},{5,7},{7,1},{8,10},{10,12},{12... | collective-permute-start | bytes 294920 | tf_op jit(solution)/shard_map/ppermute | solution.py:30
  205.0 3.1 %collective-permute-start.3 = (f32[3,32,32,8]{2,3,1,0:T(8,128)S(1)}, f32[3,32,32,8]{2,3,1,0:T(8,128)}, u32[]{:S(2)}, u32[]{:S(2)}) collective-permute-start(f32[3,32,32,8]{2,3,1,0:T(8,128)S(1)} %copy.21), channel_id=1, source_target_pairs={{2,0},{4,2},{6,4},{0,6},{3,1},{5,3},{7,5},{1,7},{10,8},{12,10},{14... | collective-permute-start | bytes 294920 | tf_op jit(solution)/shard_map/ppermute | solution.py:33
  208.1 6.5 %collective-permute-done.2 = f32[3,32,32,8]{2,3,1,0:T(8,128)S(1)} collective-permute-done((f32[3,32,32,8]{2,3,1,0:T(8,128)}, f32[3,32,32,8]{2,3,1,0:T(8,128)S(1)}, u32[]{:S(2)}, u32[]{:S(2)}) %collective-permute-start.2) | collective-permute-done | bytes 98336 | tf_op jit(solution)/shard_map/ppermute | solution.py:30
  215.1 2.0 collective-permute-done.3
  217.1 1.5 copy.19
  218.6 2.6 %pad_maximum_fusion = f32[3,32,32,144]{3,2,1,0:T(8,128)S(1)} fusion(f32[3,32,32,8]{3,2,1,0:T(8,128)S(1)} %copy.19, f32[3,32,8,128]{3,2,1,0:T(8,128)} %collective-permute-done.1, f32[1,32,16,128]{3,2,1,0:T(8,128)} %bitcast.26, f32[1,32,16,128]{3,2,1,0:T(8,128)} %bitcast.29, f32[1,32,16,128]{3,2,1,0:T(8,128)S(1)} %multiply_bitcast_fusion, ...), kind=kLoop, calls=%fused_computation | loop fusion | flops 2654208 | bytes 3538944 | tf_op jit(solution)/shard_map/concatenate | solution.py:34
  221.5 1.7 slice_multiply_fusion.3
  224.4 1.7 slice_multiply_fusion.1
  227.0 1.3 slice_multiply_fusion.7
  229.2 1.3 slice_multiply_fusion.5
  231.3 6.2 %all_to_all.5 = f32[2,3,32,16,128]{4,3,2,1,0:T(8,128)S(1)} all-to-all(f32[2,3,32,16,128]{4,3,2,1,0:T(8,128)S(1)} %broadcast_in_dim.2), channel_id=1, replica_groups=mesh['member'=2,'tile'=32,'row'=4,'lev'=2] {'lev'}, dimensions={0} | all-to-all | bytes 3145728 | tf_op jit(solution)/shard_map/all_to_all | solution.py:46
  237.7 6.9 %bitcast_subtract_fusion = f32[64,16,128]{2,1,0:T(8,128)S(1)} fusion(f32[1,2,32,16,128]{4,3,2,0,1:T(8,128)S(1)} %get-tuple-element.62, f32[64,16,128]{2,1,0:T(8,128)S(1)} %bitcast.22), kind=kOutput, calls=%fused_computation.104 | output fusion | flops 8388608 | bytes 1572864 | tf_op jit(solution)/shard_map/jit(cumsum)/reduce_window_sum | solution.py:78
  245.0 2.7 %multiply_reduce_fusion.7 = (f32[33,16,128]{2,1,0:T(8,128)S(1)}, f32[33,16,128]{2,1,0:T(8,128)S(1)}, f32[33,16,128]{2,1,0:T(8,128)S(1)}, f32[33,16,128]{2,1,0:T(...) fusion(f32[8,16,128]{2,1,0:T(8,128)S(1)} %get-tuple-element.82,, ...), kind=kLoop, calls=%fused_computation.8 | loop fusion | flops 14598144 | bytes 3481600 | tf_op jit(solution)/shard_map/reduce_sum | solution.py:88
  247.6 2.7 %multiply_reduce_fusion.6 = (f32[33,16,128]{2,1,0:T(8,128)S(1)}, f32[33,16,128]{2,1,0:T(8,128)S(1)}, f32[33,16,128]{2,1,0:T(8,128)S(1)}, f32[33,16,128]{2,1,0:T(...) fusion(f32[8,16,128]{2,1,0:T(8,128)S(1)} %get-tuple-element.81,, ...), kind=kLoop, calls=%fused_computation.7 | loop fusion | flops 14598144 | bytes 3481600 | tf_op jit(solution)/shard_map/reduce_sum | solution.py:88
  (34 shorter events, 12.2 us)
Async XLA Ops:
  0.6 197.2 %copy-start.1 = (f32[32,16,128]{2,1,0:T(8,128)S(1)}, f32[32,16,128]{2,1,0:T(8,128)}, u32[]{:S(2)}) copy-start(f32[32,16,128]{2,1,0:T(8,128)} %param.5) | copy-start | bytes 786436
  0.6 197.2 %copy-start = (f32[32,16,128]{2,1,0:T(8,128)S(1)}, f32[32,16,128]{2,1,0:T(8,128)}, u32[]{:S(2)}) copy-start(f32[32,16,128]{2,1,0:T(8,128)} %param.6) | copy-start | bytes 786436
  119.0 78.7 %collective-permute-start = (f32[3,32,8,128]{3,2,1,0:T(8,128)S(1)}, f32[3,32,8,128]{3,2,1,0:T(8,128)}, u32[]{:S(2)}, u32[]{:S(2)}) collective-permute-start(f32[3,32,8,128]{3,2,1,0:T(8,128)S(1)} %get-tuple-element.73), channel_id=1, source_target_pairs={{0,8},{8,16},{16,24},{24,32},{32,40},{40,48},{48,56},{56,64},{64,7... | collective-permute-start | bytes 1179656 | tf_op jit(solution)/shard_map/ppermute | solution.py:30
  121.0 76.8 %collective-permute-start.1 = (f32[3,32,8,128]{3,2,1,0:T(8,128)S(1)}, f32[3,32,8,128]{3,2,1,0:T(8,128)}, u32[]{:S(2)}, u32[]{:S(2)}) collective-permute-start(f32[3,32,8,128]{3,2,1,0:T(8,128)S(1)} %get-tuple-element.74), channel_id=1, source_target_pairs={{8,0},{16,8},{24,16},{32,24},{40,32},{48,40},{56,48},{64,56},{72,6... | collective-permute-start | bytes 1179656 | tf_op jit(solution)/shard_map/ppermute | solution.py:33
  200.9 13.7 %collective-permute-start.2 = (f32[3,32,32,8]{2,3,1,0:T(8,128)}, f32[3,32,32,8]{2,3,1,0:T(8,128)S(1)}, u32[]{:S(2)}, u32[]{:S(2)}) collective-permute-start(f32[3,32,32,8]{2,3,1,0:T(8,128)} %copy.20), channel_id=1, source_target_pairs={{0,2},{2,4},{4,6},{6,0},{1,3},{3,5},{5,7},{7,1},{8,10},{10,12},{12... | collective-permute-start | bytes 294920 | tf_op jit(solution)/shard_map/ppermute | solution.py:30
  205.0 12.1 %collective-permute-start.3 = (f32[3,32,32,8]{2,3,1,0:T(8,128)S(1)}, f32[3,32,32,8]{2,3,1,0:T(8,128)}, u32[]{:S(2)}, u32[]{:S(2)}) collective-permute-start(f32[3,32,32,8]{2,3,1,0:T(8,128)S(1)} %copy.21), channel_id=1, source_target_pairs={{2,0},{4,2},{6,4},{0,6},{3,1},{5,3},{7,5},{1,7},{10,8},{12,10},{14... | collective-permute-start | bytes 294920 | tf_op jit(solution)/shard_map/ppermute | solution.py:33
where the time goes:
time: 253 us; the launch traced here: 252 us
  blocking collectives  190 us (75%)
  other arithmetic  31.5 us (12%)
  starting transfers between devices  13.3 us (5%)
  waiting for transfers between devices  8.47 us (3%)
  local copies, waits for them, and re-layouts  5.87 us (2%)
  between operations  2.96 us (1%)
    psum x3, blocking collectives, over_axes(): shard = lax.psum(shard, axis)  113 us
    pmax x3, blocking collectives, one_axis_at_a_time(): shard = lax.pmax(shard, axis)  71.5 us
    ppermute x2, starting transfers between devices, padded(): lax.ppermute(lax.slice_in_dim(block, 0, width, axis=dim), axis, backward)  7.7 us
    another operation x1, other arithmetic, remap_columns(): tops = jnp.cumsum(height, 0) - height  6.88 us
    ppermute x2, waiting for transfers between devices, padded(): lax.ppermute(lax.slice_in_dim(block, block.shape[dim] - width, None, axis...  6.46 us
    all_to_all x1, blocking collectives, sent_to_all(): lax.all_to_all(jnp.broadcast_to(shard[None], (length, *shard.shape)), axi...  6.23 us
    mul x4, other arithmetic, advance(): flux_east = centre * zonal_new  5.99 us
    ppermute x2, starting transfers between devices, padded(): lax.ppermute(lax.slice_in_dim(block, block.shape[dim] - width, None, axis...  5.58 us
  transfers between devices with their start and end apart: 4, of which 2 were waited for; matrix products, arithmetic and copies ran while one was open for 0% of the time, Pallas kernels for 0%

commit v1 on v0

--- a/solution.py
+++ b/solution.py
@@ -1,6 +1,9 @@
+import functools
 import jax
 import jax.numpy as jnp
 from jax import lax
+from jax.experimental import pallas as pl
+from jax.experimental.pallas import tpu as pltpu
 from jax.sharding import PartitionSpec as P
 
 NSUB = 4
@@ -8,17 +11,131 @@
 
 CFL_NUMBER = 0.8
 
-
-def one_axis_at_a_time(shard, axes):
-    for axis in axes:
-        shard = lax.pmax(shard, axis)
-    return shard
-
-
-def over_axes(shard, axes):
-    for axis in axes:
-        shard = lax.psum(shard, axis)
-    return shard
+MESH = pl.DeviceIdType.MESH
+
+
+def combine(lane, a, b):
+    return jnp.where(lane == 0, jnp.maximum(a, b), a + b)
+
+
+def totals_kernel(
+    tiles, rows, thick_ref, codes_ref, out_ref,
+    mine, plane, near, far, got_plane, got_near, got_mid, got_far,
+    send_plane, recv_plane, send_near, recv_near, send_mid, recv_mid, send_far, recv_far,
+):
+    tile = lax.axis_index("tile")
+    row = lax.axis_index("row")
+    lev = lax.axis_index("lev")
+
+    def along(d):
+        return lax.rem(tile + (d + tiles), tiles)
+
+    def mate(dr, dl):
+        return {"row": lax.rem(row + dr, rows), "lev": lax.rem(lev + dl, 2)}
+
+    mates = [(dr, dl) for dr in range(rows) for dl in range(2) if dr or dl]
+    close = [1, -1, 2, -2, 3, -3]
+
+    barrier = pltpu.get_barrier_semaphore()
+    for dr, dl in mates:
+        pl.semaphore_signal(barrier, inc=1, device_id=mate(dr, dl), device_id_type=MESH)
+    for d in close:
+        pl.semaphore_signal(barrier, inc=1, device_id={"tile": along(d)}, device_id_type=MESH)
+
+    thick = thick_ref[...]
+    bump = 2.0 * (codes_ref[...] & 4095).astype(jnp.float32) / 4095.0
+    raised = thick + bump[None]
+
+    def folded(x, op):
+        x = op(x, axis=0)
+        x = op(x, axis=0, keepdims=True)
+        return op(x, axis=1, keepdims=True)
+
+    lane = lax.broadcasted_iota(jnp.int32, (1, 128), 1)
+    peak = folded(raised, jnp.max)
+    base = folded(thick, jnp.sum)
+    lifted = folded(raised, jnp.sum)
+    packet = jnp.where(lane == 0, peak, jnp.where(lane == 1, base, lifted))
+    mine[0] = packet
+    pl.semaphore_wait(barrier, len(mates) + len(close))
+
+    copies = []
+
+    def send(src, dst, ssem, rsem, device):
+        copy = pltpu.make_async_remote_copy(
+            src_ref=src, dst_ref=dst, send_sem=ssem, recv_sem=rsem,
+            device_id=device, device_id_type=MESH,
+        )
+        copy.start()
+        copies.append(copy)
+
+    for s, (dr, dl) in enumerate(mates):
+        send(mine.at[0], got_plane.at[s], send_plane.at[s], recv_plane.at[s], mate(dr, dl))
+    total = packet
+    for s in range(len(mates)):
+        copies[s].wait_recv()
+        total = combine(lane, total, got_plane[s])
+    plane[0] = total
+
+    first = len(copies)
+    for s, d in enumerate(close):
+        send(plane.at[0], got_near.at[s], send_near.at[s], recv_near.at[s], {"tile": along(d)})
+    held = {0: total}
+    for s, d in enumerate(close):
+        copies[first + s].wait_recv()
+        held[-d] = got_near[s]
+
+    def over(lo, hi):
+        out = held[lo]
+        for i in range(lo + 1, hi + 1):
+            out = combine(lane, out, held[i])
+        return out
+
+    up = over(-3, 2)
+    down = over(-2, 2)
+    near[0] = up
+    near[1] = jnp.where(lane < 3, down, pltpu.roll(held[3], 3, 1))
+    first = len(copies)
+    send(near.at[0], got_mid.at[0], send_mid.at[0], recv_mid.at[0], {"tile": along(6)})
+    send(near.at[1], got_mid.at[1], send_mid.at[1], recv_mid.at[1], {"tile": along(-6)})
+    copies[first].wait_recv()
+    copies[first + 1].wait_recv()
+    below = got_mid[0]
+    above = got_mid[1]
+    above_last = pltpu.roll(above, 125, 1)
+
+    far[0] = combine(lane, below, held[-3])
+    far[1] = combine(lane, above, held[3])
+    first = len(copies)
+    send(far.at[0], got_far.at[0], send_far.at[0], recv_far.at[0], {"tile": along(7)})
+    send(far.at[1], got_far.at[1], send_far.at[1], recv_far.at[1], {"tile": along(-7)})
+    inner = combine(lane, over(-3, 3), combine(lane, below, combine(lane, above, above_last)))
+    copies[first].wait_recv()
+    copies[first + 1].wait_recv()
+    out_ref[...] = combine(lane, inner, combine(lane, got_far[0], got_far[1]))
+    for copy in copies:
+        copy.wait_send()
+
+
+def totals(thickness, pert_codes):
+    tiles = lax.axis_size("tile")
+    rows = lax.axis_size("row")
+    mates = 2 * rows - 1
+    dma = pltpu.SemaphoreType.DMA
+    packets = lambda n: pltpu.VMEM((n, 1, 128), jnp.float32)
+    return pl.pallas_call(
+        functools.partial(totals_kernel, tiles, rows),
+        out_shape=jax.ShapeDtypeStruct((1, 128), jnp.float32),
+        in_specs=[pl.BlockSpec(memory_space=pltpu.VMEM)] * 2,
+        out_specs=pl.BlockSpec(memory_space=pltpu.VMEM),
+        scratch_shapes=[
+            packets(1), packets(1), packets(2), packets(2),
+            packets(mates), packets(6), packets(2), packets(2),
+            dma((mates,)), dma((mates,)), dma((6,)), dma((6,)), dma((2,)), dma((2,)), dma((2,)), dma((2,)),
+        ],
+        compiler_params=pltpu.CompilerParams(collective_id=0, has_side_effects=True),
+        name="totals",
+    )(thickness, pert_codes)
 
 
 def padded(block, sides, width):
@@ -96,14 +213,8 @@
 def local(thickness, zonal_wind, merid_wind, pert_codes):
     bump = 2.0 * (pert_codes % 4096).astype(jnp.float32) / 4095.0
     raised = thickness + bump[None]
-    local_peak = jnp.max(raised)
-    base_mass = jnp.sum(thickness)
-    raised_mass = jnp.sum(raised)
-    peak = one_axis_at_a_time(local_peak, ("tile", "row", "lev"))
-    base_total, raised_total = (
-        over_axes(base_mass, ("tile", "row", "lev")),
-        over_axes(raised_mass, ("tile", "row", "lev")),
-    )
+    sums = totals(thickness, pert_codes)
+    peak, base_total, raised_total = sums[0, 0], sums[0, 1], sums[0, 2]
     height = raised * (base_total / raised_total)
     half_step = 0.5 * CFL_NUMBER / jnp.sqrt(peak)
     state = jnp.stack([height, zonal_wind, merid_wind])

time: 253 us -> 138 us (0.55)
  blocking collectives: 190 us -> 10.6 us
  Pallas kernels: 0 us -> 65.9 us
  other arithmetic: 31.5 us -> 28.8 us
    psum x3 -> x0, blocking collectives: 113 us -> none  [over_axes(): shard = lax.psum(shard, axis)]
    pmax x3 -> x0, blocking collectives: 71.5 us -> none  [one_axis_at_a_time(): shard = lax.pmax(shard, axis)]
    pallas_call x0 -> x1, Pallas kernels: none -> 65.9 us  [totals(): pl.pallas_call(functools.partial(totals_kernel, tiles, rows), out_shape=j...]
    all_to_all x1, blocking collectives: 6.23 us -> 10.6 us  [sent_to_all(): lax.all_to_all(jnp.broadcast_to(shard[None], (length, *shard.shape)), axi...]
  transfers between devices with their start and end apart: 4 -> 4, of which waited for: 2 -> 4; matrix products, arithmetic and copies ran while one was open for 0% -> 1% of each run, Pallas kernels for 0% -> 0%
where the time goes in v1:
time: 138 us; the launch traced here: 137 us
  Pallas kernels  65.9 us (48%)
  other arithmetic  28.8 us (21%)
  starting transfers between devices  13.3 us (10%)
  blocking collectives  10.6 us (8%)
  waiting for transfers between devices  8.02 us (6%)
  local copies, waits for them, and re-layouts  8.01 us (6%)
  between operations  2.93 us (2%)
    pallas_call x1, Pallas kernels, totals(): pl.pallas_call(functools.partial(totals_kernel, tiles, rows), out_shape=j...  65.9 us
    all_to_all x1, blocking collectives, sent_to_all(): lax.all_to_all(jnp.broadcast_to(shard[None], (length, *shard.shape)), axi...  10.6 us
    ppermute x2, starting transfers between devices, padded(): lax.ppermute(lax.slice_in_dim(block, 0, width, axis=dim), axis, backward)  8.7 us
    another operation x1, other arithmetic, remap_columns(): tops = jnp.cumsum(height, 0) - height  6.88 us
    mul x4, other arithmetic, advance(): flux_east = centre * zonal_new  5.99 us
    ppermute x2, waiting for transfers between devices, padded(): lax.ppermute(lax.slice_in_dim(block, block.shape[dim] - width, None, axis...  5.97 us
    reduce_sum x2, other arithmetic, remap_columns(): merid_sum = merid_sum + jnp.sum(merid[lower:upper, None] * over, 0)  5.41 us
    ppermute x2, starting transfers between devices, padded(): lax.ppermute(lax.slice_in_dim(block, block.shape[dim] - width, None, axis...  4.58 us
  transfers between devices with their start and end apart: 4, of which 4 were waited for; matrix products, arithmetic and copies ran while one was open for 1% of the time, Pallas kernels for 0%

profile of v1, /device:TPU:33, one launch (start us, length us, event | category | flops | bytes accessed | tf_op | source)
XLA Modules:
  0.0 137.5 jit_solution(1480900633950909411)
XLA Ops:
  1.4 65.9 %totals.1 = f32[1,128]{1,0:T(1,128)} custom-call(f32[32,16,128]{2,1,0:T(8,128)} %thick_ref.1, s32[16,128]{1,0:T(8,128)} %codes_ref.1), custom_call_target="tpu_custom_call" | custom-call | tf_op jit(solution)/shard_map/totals/pallas_call | solution.py:126
  67.4 1.4 %fusion.49 = (f32[1,1]{1,0:T(1,128)}, f32[1,1]{1,0:T(1,128)}, f32[1,1]{1,0:T(1,128)}) fusion(f32[1,128]{1,0:T(1,128)} %totals.1), kind=kLoop, calls=%fused_computation.111 | loop fusion | bytes 24 | tf_op jit(solution)/shard_map/slice | solution.py:217
  70.1 1.0 multiply_bitcast_fusion
  71.1 1.1 pad_maximum_fusion.2
  72.2 2.2 %collective-permute-start = (f32[3,32,8,128]{3,2,1,0:T(8,128)S(1)}, f32[3,32,8,128]{3,2,1,0:T(8,128)S(1)}, u32[]{:S(2)}, u32[]{:S(2)}) collective-permute-start(f32[3,32,8,128]{3,2,1,0:T(8,128)S(1)} %get-tuple-element.64), channel_id=1, source_target_pairs={{0,8},{8,16},{16,24},{24,32},{32,40},{40,48},{48,56},{56,64},{64,7... | collective-permute-start | bytes 1179656 | tf_op jit(solution)/shard_map/ppermute | solution.py:147
  74.4 4.3 %collective-permute-start.1 = (f32[3,32,8,128]{3,2,1,0:T(8,128)S(1)}, f32[3,32,8,128]{3,2,1,0:T(8,128)S(1)}, u32[]{:S(2)}, u32[]{:S(2)}) collective-permute-start(f32[3,32,8,128]{3,2,1,0:T(8,128)S(1)} %get-tuple-element.65), channel_id=1, source_target_pairs={{8,0},{16,8},{24,16},{32,24},{40,32},{48,40},{56,48},{64,56},{72,6... | collective-permute-start | bytes 1179656 | tf_op jit(solution)/shard_map/ppermute | solution.py:150
  79.5 3.2 %collective-permute-done = f32[3,32,8,128]{3,2,1,0:T(8,128)S(1)} collective-permute-done((f32[3,32,8,128]{3,2,1,0:T(8,128)S(1)}, f32[3,32,8,128]{3,2,1,0:T(8,128)S(1)}, u32[]{:S(2)}, u32[]{:S(2)}) %collective-permute-start) | collective-permute-done | bytes 393248 | tf_op jit(solution)/shard_map/ppermute | solution.py:147
  85.0 1.2 copy.21
  86.2 2.4 %collective-permute-start.2 = (f32[3,32,32,8]{2,3,1,0:T(8,128)}, f32[3,32,32,8]{2,3,1,0:T(8,128)S(1)}, u32[]{:S(2)}, u32[]{:S(2)}) collective-permute-start(f32[3,32,32,8]{2,3,1,0:T(8,128)} %copy.21), channel_id=1, source_target_pairs={{0,2},{2,4},{4,6},{6,0},{1,3},{3,5},{5,7},{7,1},{8,10},{10,12},{12... | collective-permute-start | bytes 294920 | tf_op jit(solution)/shard_map/ppermute | solution.py:147
  89.0 4.4 %collective-permute-start.3 = (f32[3,32,32,8]{2,3,1,0:T(8,128)S(1)}, f32[3,32,32,8]{2,3,1,0:T(8,128)}, u32[]{:S(2)}, u32[]{:S(2)}) collective-permute-start(f32[3,32,32,8]{2,3,1,0:T(8,128)S(1)} %copy.22), channel_id=1, source_target_pairs={{2,0},{4,2},{6,4},{0,6},{3,1},{5,3},{7,5},{1,7},{10,8},{12,10},{14... | collective-permute-start | bytes 294920 | tf_op jit(solution)/shard_map/ppermute | solution.py:150
  93.4 2.8 %collective-permute-done.2 = f32[3,32,32,8]{2,3,1,0:T(8,128)S(1)} collective-permute-done((f32[3,32,32,8]{2,3,1,0:T(8,128)}, f32[3,32,32,8]{2,3,1,0:T(8,128)S(1)}, u32[]{:S(2)}, u32[]{:S(2)}) %collective-permute-start.2) | collective-permute-done | bytes 98336 | tf_op jit(solution)/shard_map/ppermute | solution.py:147
  96.6 1.3 collective-permute-done.3
  97.9 1.5 %copy.20 = f32[3,32,32,8]{3,2,1,0:T(8,128)S(1)} copy(f32[3,32,32,8]{2,3,1,0:T(8,128)} %collective-permute-done.3) | data formatting | bytes 196608 | tf_op jit(solution)/shard_map/ppermute | solution.py:150
  99.4 2.6 %pad_maximum_fusion = f32[3,32,32,144]{3,2,1,0:T(8,128)S(1)} fusion(f32[3,32,32,8]{3,2,1,0:T(8,128)S(1)} %copy.20, f32[3,32,8,128]{3,2,1,0:T(8,128)} %copy-done.3, f32[1,32,16,128]{3,2,1,0:T(8,128)} %bitcast.28, f32[1,32,16,128]{3,2,1,0:T(8,128)} %bitcast.31, f32[1,32,16,128]{3,2,1,0:T(8,128)S(1)} %multiply_bitcast_fusion, f32[3,32,8,128]{3,2,1,0:T(8,128)} %copy-done.2, ...), kind=kLoop, calls=%fused_computation | loop fusion | flops 2654208 | bytes 3538944 | tf_op jit(solution)/shard_map/concatenate | solution.py:151
  102.3 1.7 %slice_multiply_fusion.3 = (f32[32,30,142]{2,1,0:T(8,128)S(1)}, f32[32,30,142]{2,1,0:T(8,128)S(1)}, f32[32,30,142]{2,1,0:T(8,128)S(1)}, f32[32,30,142]{2,1,0:T(8,128)S(1)}) fusion(f32[32,32,144]{2,1,0:T(8,128)S(1)} %get-tuple-element.49, f32[]{:T(128)} %bitcast.5, f32[32,32,144]{2,1,0:T(8,128)S(1)} %get-tuple-element.47, f32[32,32,144]{2,1,0:T(8,128)S(1)} %get-tuple-element.48), kind=kLoop, calls=%fused_computation.49 | loop fusion | flops 1090560 | bytes 5998084 | tf_op jit(solution)/shard_map/mul | solution.py:179
  104.0 1.2 fusion.6
  105.2 1.7 %slice_multiply_fusion.1 = (f32[32,26,138]{2,1,0:T(8,128)S(1)}, f32[32,26,138]{2,1,0:T(8,128)S(1)}, f32[32,26,138]{2,1,0:T(8,128)S(1)}, f32[32,26,138]{2,1,0:T(8,128)S(1)}) fusion(f32[32,28,140]{2,1,0:T(8,128)S(1)} %fusion.6, f32[]{:T(128)} %bitcast.5, f32[32,30,142]{2,1,0:T(8,128)S(1)} %get-tuple-element.44, f32[32,30,142]{2,1,0:T(8,128)S(1)} %get-tuple-element.59), kind=kLoop, calls=%fused_computation.47 | loop fusion | flops 918528 | bytes 5051908 | tf_op jit(solution)/shard_map/mul | solution.py:179
  107.8 1.3 slice_multiply_fusion.7
  109.1 0.9 fusion.17
  110.0 1.3 slice_multiply_fusion.5
  112.2 10.6 %all_to_all.5 = f32[2,3,32,16,128]{4,3,2,1,0:T(8,128)S(1)} all-to-all(f32[2,3,32,16,128]{4,3,2,1,0:T(8,128)S(1)} %broadcast_in_dim.2), channel_id=1, replica_groups=mesh['member'=2,'tile'=32,'row'=4,'lev'=2] {'lev'}, dimensions={0} | all-to-all | bytes 3145728 | tf_op jit(solution)/shard_map/all_to_all | solution.py:163
  122.9 6.9 %bitcast_subtract_fusion = f32[64,16,128]{2,1,0:T(8,128)S(1)} fusion(f32[1,2,32,16,128]{4,3,2,0,1:T(8,128)S(1)} %get-tuple-element.53, f32[64,16,128]{2,1,0:T(8,128)S(1)} %bitcast.24), kind=kOutput, calls=%fused_computation.102 | output fusion | flops 8388608 | bytes 1572864 | tf_op jit(solution)/shard_map/jit(cumsum)/reduce_window_sum | solution.py:195
  130.1 2.7 %multiply_reduce_fusion.7 = (f32[33,16,128]{2,1,0:T(8,128)S(1)}, f32[33,16,128]{2,1,0:T(8,128)S(1)}, f32[33,16,128]{2,1,0:T(8,128)S(1)}, f32[33,16,128]{2,1,0:T(...) fusion(f32[8,16,128]{2,1,0:T(8,128)S(1)} %get-tuple-element.73,, ...), kind=kLoop, calls=%fused_computation.8 | loop fusion | flops 14598144 | bytes 3481600 | tf_op jit(solution)/shard_map/reduce_sum | solution.py:205
  132.8 2.7 %multiply_reduce_fusion.6 = (f32[33,16,128]{2,1,0:T(8,128)S(1)}, f32[33,16,128]{2,1,0:T(8,128)S(1)}, f32[33,16,128]{2,1,0:T(8,128)S(1)}, f32[33,16,128]{2,1,0:T(...) fusion(f32[8,16,128]{2,1,0:T(8,128)S(1)} %get-tuple-element.72,, ...), kind=kLoop, calls=%fused_computation.7 | loop fusion | flops 14598144 | bytes 3481600 | tf_op jit(solution)/shard_map/reduce_sum | solution.py:205
  (33 shorter events, 8.5 us)
Async XLA Ops:
  0.6 83.6 %copy-start.1 = (f32[32,16,128]{2,1,0:T(8,128)S(1)}, f32[32,16,128]{2,1,0:T(8,128)}, u32[]{:S(2)}) copy-start(f32[32,16,128]{2,1,0:T(8,128)} %param.5) | copy-start | bytes 786436
  0.6 83.6 %copy-start = (f32[32,16,128]{2,1,0:T(8,128)S(1)}, f32[32,16,128]{2,1,0:T(8,128)}, u32[]{:S(2)}) copy-start(f32[32,16,128]{2,1,0:T(8,128)} %param.6) | copy-start | bytes 786436
  72.2 10.5 %collective-permute-start = (f32[3,32,8,128]{3,2,1,0:T(8,128)S(1)}, f32[3,32,8,128]{3,2,1,0:T(8,128)S(1)}, u32[]{:S(2)}, u32[]{:S(2)}) collective-permute-start(f32[3,32,8,128]{3,2,1,0:T(8,128)S(1)} %get-tuple-element.64), channel_id=1, source_target_pairs={{0,8},{8,16},{16,24},{24,32},{32,40},{40,48},{48,56},{56,64},{64,7... | collective-permute-start | bytes 1179656 | tf_op jit(solution)/shard_map/ppermute | solution.py:147
  74.4 9.0 %collective-permute-start.1 = (f32[3,32,8,128]{3,2,1,0:T(8,128)S(1)}, f32[3,32,8,128]{3,2,1,0:T(8,128)S(1)}, u32[]{:S(2)}, u32[]{:S(2)}) collective-permute-start(f32[3,32,8,128]{3,2,1,0:T(8,128)S(1)} %get-tuple-element.65), channel_id=1, source_target_pairs={{8,0},{16,8},{24,16},{32,24},{40,32},{48,40},{56,48},{64,56},{72,6... | collective-permute-start | bytes 1179656 | tf_op jit(solution)/shard_map/ppermute | solution.py:150
  82.7 0.8 copy-start.2
  83.5 0.7 copy-start.3
  86.2 10.0 %collective-permute-start.2 = (f32[3,32,32,8]{2,3,1,0:T(8,128)}, f32[3,32,32,8]{2,3,1,0:T(8,128)S(1)}, u32[]{:S(2)}, u32[]{:S(2)}) collective-permute-start(f32[3,32,32,8]{2,3,1,0:T(8,128)} %copy.21), channel_id=1, source_target_pairs={{0,2},{2,4},{4,6},{6,0},{1,3},{3,5},{5,7},{7,1},{8,10},{10,12},{12... | collective-permute-start | bytes 294920 | tf_op jit(solution)/shard_map/ppermute | solution.py:147
  89.0 8.9 %collective-permute-start.3 = (f32[3,32,32,8]{2,3,1,0:T(8,128)S(1)}, f32[3,32,32,8]{2,3,1,0:T(8,128)}, u32[]{:S(2)}, u32[]{:S(2)}) collective-permute-start(f32[3,32,32,8]{2,3,1,0:T(8,128)S(1)} %copy.22), channel_id=1, source_target_pairs={{2,0},{4,2},{6,4},{0,6},{3,1},{5,3},{7,5},{1,7},{10,8},{12,10},{14... | collective-permute-start | bytes 294920 | tf_op jit(solution)/shard_map/ppermute | solution.py:150
